TPU v7x, 32 devices: a whole 2x2x4 slice. The times are simulated.
32 devices in a mesh: vocab: 4 (over x, core), section: 2 (over y), dp: 4 (over z).
Axes of the slice: x: 2, y: 2, z: 4, core: 2. Of those that a mesh axis runs over, the one named last changes fastest.
Arguments:
- teacher_hidden: bfloat16 [128, 16384], P(('dp', 'vocab', 'section')), parts along dimension 0, may hold values from -12 to 12
- student_hidden: bfloat16 [128, 8192], P(('dp', 'vocab', 'section')), parts along dimension 0, may hold values from -12 to 12
- teacher_head: bfloat16 [16384, 2048], P(None, ('vocab', 'section')), may hold values from -0.051452637 to 0.051452637
- student_head: bfloat16 [8192, 2048], P(None, ('vocab', 'section')), may hold values from -0.07544653 to 0.07544653
- token_weight: float32 [128], P('dp'), parts along dimension 0, may hold values from 1 to 30
Outputs:
- token_kl: float32 [128], P(('dp', 'vocab', 'section')), parts along dimension 0
- hidden_grad: float32 [128, 8192], P(('dp', 'vocab', 'section')), parts along dimension 0
There are 4 independent parts, one for each index of `dp`. A program takes and returns all parts, laid end to end along the dimension named above; an argument that names none is the same for every part. Nothing has to cross between parts.
All inputs are finite; a program needn't handle non-finite values.
Results may differ from a plain program's by a relative error of at most 0.0042.
Values may be sent and summed in bfloat16 or wider, within the bound.
A program may use at most 128 MiB of HBM per device.

v0:
```python
import jax
import jax.numpy as jnp
from jax import lax
from jax.sharding import PartitionSpec as P


def merged(value, axis, join):
    pieces = jax.tree.map(lambda part: lax.all_gather(part, axis), value)
    head = jax.tree.map(lambda part: part[0], pieces)
    tail = jax.tree.map(lambda part: part[1:], pieces)
    total, _ = lax.scan(lambda total, section: (join(total, section), None), head, tail)
    return total


def combine_parts(first, second):
    t_first, s_first, tt_first, st_first, c_first = first
    t_second, s_second, tt_second, st_second, c_second = second
    t_max = jnp.maximum(t_first, t_second)
    s_max = jnp.maximum(s_first, s_second)
    t_scale_a = jnp.exp(t_first - t_max)
    t_scale_b = jnp.exp(t_second - t_max)
    s_scale_a = jnp.exp(s_first - s_max)
    s_scale_b = jnp.exp(s_second - s_max)
    return (
        t_max,
        s_max,
        tt_first * t_scale_a + tt_second * t_scale_b,
        st_first * s_scale_a + st_second * s_scale_b,
        c_first * t_scale_a + c_second * t_scale_b,
    )


def shards(teacher_hidden, student_hidden, teacher_head, student_head, token_weight):
    teacher_logits = jnp.dot(
        lax.all_gather(teacher_hidden, ("vocab", "section"), axis=0, tiled=True),
        teacher_head,
        preferred_element_type=jnp.float32,
    )
    student_logits = jnp.dot(
        lax.all_gather(student_hidden, ("vocab", "section"), axis=0, tiled=True),
        student_head,
        preferred_element_type=jnp.float32,
    )
    local_tmax = jnp.max(teacher_logits, axis=1)
    local_smax = jnp.max(student_logits, axis=1)
    local_texp = jnp.exp(teacher_logits - local_tmax[:, None])
    local_sexp = jnp.exp(student_logits - local_smax[:, None])
    parts = (
        local_tmax,
        local_smax,
        jnp.sum(local_texp, axis=1),
        jnp.sum(local_sexp, axis=1),
        jnp.sum(local_texp * (teacher_logits - student_logits), axis=1),
    )
    teacher_max, student_max, teacher_total, student_total, cross = merged(
        parts, ("vocab", "section"), combine_parts
    )
    teacher_lse = teacher_max + jnp.log(teacher_total)
    student_lse = student_max + jnp.log(student_total)
    kl_whole = cross / teacher_total - teacher_lse + student_lse
    diff = jnp.exp(student_logits - student_lse[:, None]) - jnp.exp(
        teacher_logits - teacher_lse[:, None]
    )
    logit_grad = (token_weight[:, None] * diff).astype(jnp.bfloat16)
    own_rows = teacher_hidden.shape[0]
    hidden_grad = lax.psum_scatter(
        lax.dot_general(
            logit_grad, student_head, (((1,), (1,)), ((), ())), preferred_element_type=jnp.float32
        ),
        ("vocab", "section"),
        scatter_dimension=0,
        tiled=True,
    )
    position = lax.axis_index(("vocab", "section"))
    token_kl = lax.dynamic_slice_in_dim(kl_whole, position * own_rows, own_rows, 0)
    return (token_kl, hidden_grad)


def solution(mesh):
    in_specs = (
        P(("dp", "vocab", "section"), None),
        P(("dp", "vocab", "section"), None),
        P(None, ("vocab", "section")),
        P(None, ("vocab", "section")),
        P("dp"),
    )
    out_specs = (P(("dp", "vocab", "section")), P(("dp", "vocab", "section"), None))
    return jax.shard_map(shards, mesh=mesh, in_specs=in_specs, out_specs=out_specs, check_vma=False)
```

profile of v0, /device:TPU:0, one launch (start us, length us, event | category | flops | bytes accessed | tf_op | source)
XLA Modules:
  0.0 129.6 jit_solution(13906086431021119082)
XLA Ops:
  7.2 0.7 all-gather.9.cloned.1.call-update
  8.0 19.2 %all-gather.6 = bf16[8,4,8192]{2,1,0:T(4,128)(2,1)S(1)} all-gather(bf16[1,4,8192]{2,1,0:T(4,128)(2,1)} %bitcast.48), channel_id=1, replica_groups=mesh['vocab'=4,'section'=2,'dp'=4] {'vocab','section'}, dimensions={0}, use_global_device_ids=true | all-gather | bytes 589824 | tf_op jit(solution)/shard_map/all_gather | solution.py:40
  27.2 0.1 reshape.47
  27.3 1.3 %fusion.20 = (u32[1]{0:T(128)}, u32[1]{0:T(128)}) fusion(u32[32]{0:T(128)} %constant.37, u32[]{:T(128)S(6)} %add.45, u32[]{:T(128)S(6)} %add.34), kind=kLoop, calls=%fused_computation.33 | loop fusion | bytes 24
  29.2 3.3 %fusion.22 = (f32[32]{0:T(128)S(1)}, f32[32,256]{1,0:T(8,128)S(1)}) fusion(bf16[32,8192]{1,0:T(8,128)(2,1)S(1)} %reshape.47, bf16[8192,256]{1,0:T(8,128)(2,1)} %param.10), kind=kOutput, calls=%fused_computation.35 | convolution fusion | flops 134225888 | bytes 4751488 | tf_op jit(solution)/shard_map/dot_general | solution.py:39
  32.5 0.2 dynamic-update-slice.1
  32.7 4.1 %all-gather.9.cloned.1.call-done = bf16[8,4,16384]{2,1,0:T(4,128)(2,1)} async-done(((bf16[1,4,16384]{2,1,0:T(4,128)(2,1)}), bf16[8,4,16384]{2,1,0:T(4,128)(2,1)}) %all-gather.9.cloned.1.call-update) | async-done | bytes 1048592 | tf_op jit(solution)/shard_map/all_gather | solution.py:35
  36.8 1.3 %reshape.45 = bf16[32,16384]{1,0:T(8,128)(2,1)S(1)} reshape(bf16[8,4,16384]{2,1,0:T(4,128)(2,1)} %all-gather.9.cloned.1.call-done) | data formatting | bytes 2097152
  38.2 5.0 %fusion.21 = (f32[32]{0:T(128)S(1)}, f32[32,256]{1,0:T(8,128)S(1)}) fusion(bf16[32,16384]{1,0:T(8,128)(2,1)S(1)} %reshape.45, bf16[16384,256]{1,0:T(8,128)(2,1)} %param.9), kind=kOutput, calls=%fused_computation.34 | convolution fusion | flops 268443616 | bytes 9470080 | tf_op jit(solution)/shard_map/dot_general | solution.py:34
  43.2 0.2 dynamic-update-slice
  43.5 0.2 multiply_reduce_fusion
  43.7 0.2 dynamic-update-slice.2
  43.9 0.2 dynamic-update-slice.3
  44.1 0.2 dynamic-update-slice.4
  44.4 13.6 %all-reduce.6 = (f32[256]{0:T(256)S(1)}, f32[256]{0:T(256)S(1)}, f32[256]{0:T(256)S(1)}, f32[256]{0:T(256)S(1)}, f32[256]{0:T(256)S(1)}) all-reduce(f32[256]{0:T(256)S(1)} %dynamic-update-slice, f32[256]{0:T(256)S(1)} %dynamic-update-slice.1, ...), channel_id=2, replica_groups=mesh['vocab'=4,'section'=2,'dp'=4] {'vocab','section'}, use_global_device_ids=true, to_apply=%add | all-reduce | flops 1280 | bytes 10240
  58.4 0.1 reshape.24
  58.5 0.1 reshape.25
  58.5 0.1 reshape.26
  58.6 0.1 reshape.27
  58.8 0.6 while.18
  59.4 4.6 %fusion.14 = f32[32,8192]{1,0:T(8,128)} fusion(bf16[8192,256]{1,0:T(8,128)(2,1)} %param.10, f32[32,256]{1,0:T(8,128)S(1)} %get-tuple-element.109, f32[32,256]{1,0:T(8,128)S(1)} %get-tuple-element.111, f32[32]{0:T(128)S(1)} %get-tuple-element.103, f32[32]{0:T(128)S(1)} %get-tuple-element.104, f32[32]{0:T(128)S(1)} %copy-done), kind=kOutput, calls=%fused_computation.25 | convolution fusion | flops 134258688 | bytes 5308800 | tf_op jit(solution)/shard_map/dot_general | solution.py:67
  64.6 0.6 dynamic_slice.19
  65.2 55.9 %all-reduce.9.cloned.1.call-done = f32[32,8192]{1,0:T(8,128)} async-done(((f32[32,8192]{1,0:T(8,128)}), f32[32,8192]{1,0:T(8,128)}) %all-reduce.9.cloned.1.call-update) | async-done | bytes 1048592
  121.1 1.6 %constant_dynamic-slice_fusion.5 = f32[4,8192]{1,0:T(4,128)} fusion(f32[32,8192]{1,0:T(8,128)} %all-reduce.9.cloned.1.call-done, u32[]{:T(128)S(6)} %multiply.16), kind=kLoop, calls=%fused_computation.29 | loop fusion | bytes 262148
  (43 shorter events, 1.0 us)
Async XLA Ops:
  7.2 29.7 %all-gather.9.cloned.1.call-start = ((), (), s32[]{:S(2)}) async-start(), calls=%async_computation | async-start | bytes 1179648 | tf_op jit(solution)/shard_map/all_gather | solution.py:35
  7.9 113.2 %all-reduce.9.cloned.1.call-start = ((), (), s32[]{:S(2)}) async-start(), calls=%async_computation.1 | async-start | bytes 2097152
  38.2 21.2 %copy-start = (f32[32]{0:T(128)S(1)}, f32[32]{0:T(128)}, u32[]{:S(2)}) copy-start(f32[32]{0:T(128)} %param.11) | copy-start | bytes 388
Sparse Core Ops, SparseCore 0:
  9.9 26.9 all-gather.8
  64.1 56.9 all-reduce.8
where the time goes:
time: 130 us
  waiting for transfers between devices  60.7 us (47%)
  blocking collectives  32.8 us (25%)
  between operations  15.4 us (12%)
  matrix products  12.9 us (10%)
  local copies, waits for them, and re-layouts  6.91 us (5%)
    unnamed x3, waiting for transfers between devices  56.6 us
    all_gather x1, blocking collectives, shards(): lax.all_gather(student_hidden, ('vocab', 'section'), axis=0, tiled=True)  19.2 us
    unnamed x1, blocking collectives  13.6 us
    unnamed x16, local copies, waits for them, and re-layouts  5.56 us
    dot_general x1, matrix products, shards(): jnp.dot(lax.all_gather(teacher_hidden, ('vocab', 'section'), axis=0, tile...  5.03 us
    dot_general x1, matrix products, shards(): lax.dot_general(logit_grad, student_head, (((1,), (1,)), ((), ())), prefe...  4.56 us
    all_gather x1, waiting for transfers between devices, shards(): lax.all_gather(teacher_hidden, ('vocab', 'section'), axis=0, tiled=True)  4.09 us
    dot_general x1, matrix products, shards(): jnp.dot(lax.all_gather(student_hidden, ('vocab', 'section'), axis=0, tile...  3.29 us
  transfers between devices with their start and end apart: 2, of which 2 were waited for; matrix products, arithmetic and copies ran while one was open for 4% of the time, Pallas kernels for 0%

commit v1 on v0

v1 whole, which is shorter than its diff:
```python
import functools

import jax
import jax.numpy as jnp
from jax import lax
from jax.experimental import pallas as pl
from jax.experimental.pallas import tpu as pltpu
from jax.sharding import PartitionSpec as P

CORES = 2
PACK = 16
BLOCK = 8
F32 = jnp.float32


def kernel(
    dims,
    th_hbm,
    sh_hbm,
    tw_ref,
    thead_hbm,
    shead_hbm,
    kl_ref,
    grad_ref,
    th_in,
    sh_in,
    thead,
    shead,
    phead,
    gt,
    gs,
    acc_t,
    acc_s,
    logits,
    plogits,
    stats,
    part,
    sbuf,
    rbuf,
    fbuf,
    pbuf,
    in_sem,
    thead_sem,
    phead_sem,
    send_sem,
    piece_sem,
    pair_sem,
    logit_sem,
    stat_sem,
    red_sem,
    fin_sem,
):
    n1, n2, chunks, red_width = dims
    nchips = n1 * n2
    n = nchips * CORES
    rows, kt = th_in.shape
    ks = sh_in.shape[1]
    fold = PACK // rows
    tokens = n * rows
    pair_rows = CORES * rows
    half = ks // CORES
    width = stats.shape[2]

    position, s = lax.axis_index("vocab"), lax.axis_index("section")
    v, c = position // CORES, position % CORES
    other = 1 - c
    chip = v * n2 + s
    slot = chip * CORES + c

    def device(v, s, c):
        return {"vocab": v * CORES + c, "section": s}

    sends = []

    def push(src, dst, recv, target):
        copy = pltpu.make_async_remote_copy(
            src_ref=src,
            dst_ref=dst,
            send_sem=send_sem.at[len(sends)],
            recv_sem=recv,
            device_id=target,
            device_id_type=pl.DeviceIdType.MESH,
        )
        copy.start()
        sends.append(copy)

    def arrive(dst, recv):
        pltpu.make_async_remote_copy(
            src_ref=dst,
            dst_ref=dst,
            send_sem=send_sem.at[0],
            recv_sem=recv,
            device_id=device(v, s, other),
            device_id_type=pl.DeviceIdType.MESH,
        ).wait_recv()

    barrier = pltpu.get_barrier_semaphore()
    for dv in range(n1):
        for ds in range(n2):
            for dc in range(CORES):
                if dv or ds or dc:
                    pl.semaphore_signal(
                        barrier,
                        inc=1,
                        device_id=device((v + dv) % n1, (s + ds) % n2, (c + dc) % CORES),
                        device_id_type=pl.DeviceIdType.MESH,
                    )
    load_t = pltpu.make_async_copy(th_hbm, th_in, in_sem.at[0])
    load_s = pltpu.make_async_copy(sh_hbm, sh_in, in_sem.at[1])
    load_t.start()
    load_s.start()
    loads = {}
    for index, (is_teacher, first, size, _) in enumerate(chunks):
        src, dst = (thead_hbm, thead) if is_teacher else (shead_hbm, shead)
        depth = (kt if is_teacher else ks) // fold
        for q in range(fold):
            span = pl.ds(q * depth + first, size)
            copy = pltpu.make_async_copy(src.at[span], dst.at[span], thead_sem.at[index, q])
            copy.start()
            loads[index, q] = copy

    load_t.wait()
    load_s.wait()
    for src, dst in ((th_in, gt), (sh_in, gs)):
        depth = src.shape[1] // fold
        dst[slot] = jnp.concatenate(
            [src[:, q * depth : (q + 1) * depth] for q in range(fold)], axis=0
        )
    row = lax.broadcasted_iota(jnp.int32, (tokens, width), 0)
    lane = lax.broadcasted_iota(jnp.int32, (tokens, width), 1)
    eye = row == lane
    row_chip, row_core, row_token = row // pair_rows, row % pair_rows // rows, row % rows
    source = ((row_chip // n2 * CORES + row_core) * n2 + row_chip % n2) * rows + row_token
    weight = jnp.sum(
        jnp.where(source == lane, jnp.broadcast_to(tw_ref[...], (tokens, width)), 0.0),
        axis=1,
        keepdims=True,
    )
    pl.semaphore_wait(barrier, n - 1)

    def piece(index, where, h):
        is_teacher, first, size, _ = chunks[index]
        buf = gt if is_teacher else gs
        return buf.at[where, :, pl.ds(first + h * (size // 2), size // 2)]

    def whole(index, where):
        is_teacher, first, size, _ = chunks[index]
        buf = gt if is_teacher else gs
        return buf.at[where, :, pl.ds(first, size)]

    def slot_of(v, s, c):
        return (v * n2 + s) * CORES + c

    count = len(chunks)
    along_v = [(v + dv) % n1 for dv in range(1, n1)]
    along_s = [(s + ds) % n2 for ds in range(1, n2)]
    for i in range(count):
        for h in range(2):
            ref, sem = piece(i, slot, h), piece_sem.at[2 * i + h, slot]
            first = [device(to, s, c) for to in along_v]
            second = [device(v, to, c) for to in along_s]
            for target in first + second:
                push(ref, ref, sem, target)
        push(whole(i, slot), whole(i, slot), pair_sem.at[i, slot], device(v, s, other))
    push(
        shead_hbm.at[pl.ds(pl.multiple_of(other * half, half), half)],
        phead,
        phead_sem,
        device(v, s, other),
    )
    for i in range(count):
        for h in range(2):
            for frm in along_v:
                at = slot_of(frm, s, c)
                ref, sem = piece(i, at, h), piece_sem.at[2 * i + h, at]
                arrive(ref, sem)
                if h == 0:
                    for to in along_s:
                        push(ref, ref, sem, device(v, to, c))
            for frm in along_s:
                at = slot_of(v, frm, c)
                ref, sem = piece(i, at, h), piece_sem.at[2 * i + h, at]
                arrive(ref, sem)
                if h == 1:
                    for to in along_v:
                        push(ref, ref, sem, device(to, s, c))
        for at in [slot_of(frm, s, c) for frm in along_v] + [slot_of(v, frm, c) for frm in along_s]:
            push(whole(i, at), whole(i, at), pair_sem.at[i, at], device(v, s, other))

    block = min(BLOCK, n)
    row_part = lax.broadcasted_iota(jnp.int32, (block * PACK, acc_t.shape[1]), 0) % PACK // rows
    for i in range(count):
        for fv in along_v:
            for fs in along_s:
                at = slot_of(fv, fs, c)
                for h in range(2):
                    arrive(piece(i, at, h), piece_sem.at[2 * i + h, at])
                push(whole(i, at), whole(i, at), pair_sem.at[i, at], device(v, s, other))
        for fv in range(n1):
            for fs in range(n2):
                at = slot_of((v + fv) % n1, (s + fs) % n2, other)
                arrive(whole(i, at), pair_sem.at[i, at])
        for q in range(fold):
            loads[i, q].wait()
        is_teacher, first, size, fresh = chunks[i]
        buf, head, acc = (gt, thead, acc_t) if is_teacher else (gs, shead, acc_s)
        depth = (kt if is_teacher else ks) // fold

        def multiply(b):
            lhs = buf[pl.ds(b * block, block), :, first : first + size].reshape(block * PACK, size)
            total = None
            for q in range(fold):
                rhs = head[q * depth + first : q * depth + first + size, :]
                product = jnp.dot(lhs, rhs, preferred_element_type=F32)
                total = product if total is None else jnp.where(row_part == q, product, total)
            where = pl.ds(b * block * PACK, block * PACK)
            acc[where, :] = total if fresh else acc[where, :] + total

        if n > block:
            pl.loop(0, n // block)(multiply)
        else:
            multiply(0)

    def compact(acc):
        cols = acc.shape[1]
        x = acc[...].reshape(n, PACK // 8, 8, cols)
        total = x[:, 0] + x[:, 1]
        total = total + jnp.concatenate([total[:, rows:], total[:, :rows]], axis=1)
        total = total.reshape(nchips, CORES, 8, cols)
        sub = lax.broadcasted_iota(jnp.int32, (nchips, 8, cols), 1)
        return jnp.where(sub < rows, total[:, 0], total[:, 1]).reshape(tokens, cols)

    tl, sl = compact(acc_t), compact(acc_s)
    logits[0] = tl
    logits[1] = sl
    push(logits, plogits, logit_sem, device(v, s, other))
    tmax = jnp.max(tl, axis=1, keepdims=True)
    smax = jnp.max(sl, axis=1, keepdims=True)
    texp = jnp.exp(tl - tmax)
    columns = (
        tmax,
        smax,
        jnp.sum(texp, axis=1, keepdims=True),
        jnp.sum(jnp.exp(sl - smax), axis=1, keepdims=True),
        jnp.sum(texp * (tl - sl), axis=1, keepdims=True),
    )
    lines = [jnp.sum(jnp.where(eye, col, 0.0), axis=0, keepdims=True) for col in columns]
    lines.append(jnp.zeros((8 - len(lines), width), F32))
    stats[slot] = jnp.concatenate(lines, axis=0)
    for dv in reversed(range(n1)):
        for ds in reversed(range(n2)):
            for dc in range(CORES):
                if dv or ds or dc:
                    to = device((v + dv) % n1, (s + ds) % n2, (c + dc) % CORES)
                    push(stats.at[slot], stats.at[slot], stat_sem.at[slot], to)
    for dv in range(n1):
        for ds in range(n2):
            for dc in range(CORES):
                if dv or ds or dc:
                    at = slot_of((v + dv) % n1, (s + ds) % n2, (c + dc) % CORES)
                    arrive(stats.at[at], stat_sem.at[at])
    arrive(plogits, logit_sem)
    arrive(phead, phead_sem)
    allstats = stats[...]
    tm, sm = allstats[:, 0], allstats[:, 1]
    tmax = jnp.max(tm, axis=0, keepdims=True)
    smax = jnp.max(sm, axis=0, keepdims=True)
    tscale = jnp.exp(tm - tmax)
    ttotal = jnp.sum(allstats[:, 2] * tscale, axis=0, keepdims=True)
    stotal = jnp.sum(allstats[:, 3] * jnp.exp(sm - smax), axis=0, keepdims=True)
    cross = jnp.sum(allstats[:, 4] * tscale, axis=0, keepdims=True)
    tlse = tmax + jnp.log(ttotal)
    slse = smax + jnp.log(stotal)
    kl = cross / ttotal - tlse + slse

    def column(line):
        return jnp.sum(
            jnp.where(eye, jnp.broadcast_to(line, (tokens, width)), 0.0), axis=1, keepdims=True
        )

    tlse, slse = column(tlse), column(slse)
    grads = []
    for ref in (logits, plogits):
        diff = jnp.exp(ref[1] - slse) - jnp.exp(ref[0] - tlse)
        grads.append((weight * diff).astype(jnp.bfloat16))

    steps = half // red_width
    nt = (((1,), (1,)), ((), ()))
    for j in range(steps):
        mine = pl.ds(pl.multiple_of(c * half + j * red_width, red_width), red_width)
        total = lax.dot_general(grads[0], shead[mine, :], nt, preferred_element_type=F32)
        total += lax.dot_general(
            grads[1],
            phead[j * red_width : (j + 1) * red_width, :],
            nt,
            preferred_element_type=F32,
        )
        total = total.reshape(nchips, pair_rows, red_width)
        part[:, :, j * red_width : (j + 1) * red_width] = total
        packed = jnp.concatenate(
            [total[:, :, : red_width // 2], total[:, :, red_width // 2 :]], axis=1
        )
        sbuf[:, j] = packed.astype(jnp.bfloat16)
        for dv in reversed(range(n1)):
            for ds in reversed(range(n2)):
                if dv or ds:
                    tv, ts = (v + dv) % n1, (s + ds) % n2
                    push(
                        sbuf.at[tv * n2 + ts, j],
                        rbuf.at[chip, j],
                        red_sem.at[chip, j],
                        device(tv, ts, c),
                    )

    kl_rows = column(kl)
    kl_ref[...] = jnp.sum(jnp.where(row == slot * rows + lane, kl_rows, 0.0), axis=0, keepdims=True)[
        :, :rows
    ]

    def pick(value, which):
        return jnp.where(which == 0, value[:rows], value[rows:])

    for j in range(steps):
        total = part[chip, :, j * red_width : (j + 1) * red_width]
        for dv in range(n1):
            for ds in range(n2):
                if dv or ds:
                    at = (v + dv) % n1 * n2 + (s + ds) % n2
                    arrive(rbuf.at[at, j], red_sem.at[at, j])
                    got = rbuf[at, j].astype(F32)
                    total += jnp.concatenate([got[:pair_rows], got[pair_rows:]], axis=1)
        fbuf[j] = total
        push(fbuf.at[j], pbuf.at[j], fin_sem.at[j], device(v, s, other))
        to = pl.multiple_of(c * half + j * red_width, red_width)
        grad_ref[:, pl.ds(to, red_width)] = pick(total, c)
    for j in range(steps):
        arrive(pbuf.at[j], fin_sem.at[j])
        to = pl.multiple_of(other * half + j * red_width, red_width)
        grad_ref[:, pl.ds(to, red_width)] = pick(pbuf[j], c)
    for copy in sends:
        copy.wait_send()


def shards(n1, n2, th, sh, thead, shead, tw):
    nchips = n1 * n2
    n = nchips * CORES
    rows, kt = th.shape
    ks = sh.shape[1]
    cols = thead.shape[1]
    fold = PACK // rows
    tokens = n * rows
    width = -(-tokens // 128) * 128
    td, sd = kt // fold, ks // fold
    chunks = (
        (True, 0, td // 2, True),
        (True, td // 2, td // 2, False),
        (False, 0, sd, True),
    )
    half = ks // CORES
    steps = 4
    red_width = half // steps
    count = len(chunks)
    own = (n1 - 1) + (n2 - 1)
    diagonal = (n1 - 1) * (n2 - 1)
    n_sends = (
        count * (2 * own + 2 * diagonal + nchips) + 2 + (n - 1) + steps * (nchips - 1) + steps
    )
    line = jnp.pad(tw.reshape(1, tokens), ((0, 0), (0, width - tokens)))
    vmem, anywhere = pl.BlockSpec(memory_space=pltpu.VMEM), pl.BlockSpec(memory_space=pl.ANY)
    dma = pltpu.SemaphoreType.DMA
    bf16 = jnp.bfloat16
    kl, grad = pl.pallas_call(
        functools.partial(kernel, (n1, n2, chunks, red_width)),
        out_shape=(
            jax.ShapeDtypeStruct((1, rows), F32),
            jax.ShapeDtypeStruct((rows, ks), F32),
        ),
        in_specs=[anywhere, anywhere, vmem, anywhere, anywhere],
        out_specs=(vmem, vmem),
        scratch_shapes=[
            pltpu.VMEM((rows, kt), bf16),
            pltpu.VMEM((rows, ks), bf16),
            pltpu.VMEM((kt, cols), bf16),
            pltpu.VMEM((ks, cols), bf16),
            pltpu.VMEM((half, cols), bf16),
            pltpu.VMEM((n, PACK, td), bf16),
            pltpu.VMEM((n, PACK, sd), bf16),
            pltpu.VMEM((n * PACK, cols), F32),
            pltpu.VMEM((n * PACK, cols), F32),
            pltpu.VMEM((2, tokens, cols), F32),
            pltpu.VMEM((2, tokens, cols), F32),
            pltpu.VMEM((n, 8, width), F32),
            pltpu.VMEM((nchips, CORES * rows, half), F32),
            pltpu.VMEM((nchips, steps, PACK, red_width // 2), bf16),
            pltpu.VMEM((nchips, steps, PACK, red_width // 2), bf16),
            pltpu.VMEM((steps, CORES * rows, red_width), F32),
            pltpu.VMEM((steps, CORES * rows, red_width), F32),
            dma((2,)),
            dma((count, fold)),
            dma,
            dma((n_sends,)),
            dma((2 * count, n)),
            dma((count, n)),
            dma,
            dma((n,)),
            dma((nchips, steps)),
            dma((steps,)),
        ],
        compiler_params=pltpu.CompilerParams(
            collective_id=0, has_side_effects=True, vmem_limit_bytes=60 * 1024 * 1024
        ),
    )(th, sh, line, thead, shead)
    return kl.reshape(rows), grad


def solution(mesh):
    n1, n2 = mesh.shape["vocab"] // CORES, mesh.shape["section"]
    in_specs = (
        P(("dp", "vocab", "section"), None),
        P(("dp", "vocab", "section"), None),
        P(None, ("vocab", "section")),
        P(None, ("vocab", "section")),
        P("dp"),
    )
    out_specs = (P(("dp", "vocab", "section")), P(("dp", "vocab", "section"), None))
    return jax.shard_map(
        functools.partial(shards, n1, n2),
        mesh=mesh,
        in_specs=in_specs,
        out_specs=out_specs,
        check_vma=False,
    )
```

time: 130 us -> 35.8 us (0.28)
  waiting for transfers between devices: 60.7 us -> 0 us
  blocking collectives: 32.8 us -> 0 us
  Pallas kernels: 0 us -> 31.1 us
  between operations: 15.4 us -> 0.64 us
  matrix products: 12.9 us -> 0 us
  local copies, waits for them, and re-layouts: 6.91 us -> 3.91 us
    unnamed x3 -> x0, waiting for transfers between devices: 56.6 us -> none
    pallas_call x0 -> x1, Pallas kernels: none -> 31.1 us  [shards(): pl.pallas_call(functools.partial(kernel, (n1, n2, chunks, red_width)), ou...]
    all_gather x1 -> x0, blocking collectives: 19.2 us -> none  [shards(): lax.all_gather(student_hidden, ('vocab', 'section'), axis=0, tiled=True)]
    unnamed x1 -> x0, blocking collectives: 13.6 us -> none
    dot_general x3 -> x0, matrix products: 12.9 us -> none  [the longest x1 5.03 us: shards(): jnp.dot(lax.all_gather(teacher_hidden, ('vocab', 'section'), axis=0, tile...]
    all_gather x1 -> x0, waiting for transfers between devices: 4.09 us -> none  [shards(): lax.all_gather(teacher_hidden, ('vocab', 'section'), axis=0, tiled=True)]
    unnamed x16 -> x2, local copies, waits for them, and re-layouts: 5.56 us -> 2.74 us
  transfers between devices with their start and end apart: 2 -> 0, of which waited for: 2 -> 0; matrix products, arithmetic and copies ran while one was open for 4% -> 0% of each run, Pallas kernels for 0% -> 0%
where the time goes in v1:
time: 35.8 us; the launch traced here: 35.6 us
  Pallas kernels  31.1 us (87%)
  local copies, waits for them, and re-layouts  3.91 us (11%)
  between operations  0.64 us (2%)
    pallas_call x1, Pallas kernels, shards(): pl.pallas_call(functools.partial(kernel, (n1, n2, chunks, red_width)), ou...  31.1 us
    unnamed x2, local copies, waits for them, and re-layouts  2.74 us
    pad x1, local copies, waits for them, and re-layouts, shards(): line = jnp.pad(tw.reshape(1, tokens), ((0, 0), (0, width - tokens)))  1.17 us

profile of v1, /device:TPU:0, one launch (start us, length us, event | category | flops | bytes accessed | tf_op | source)
XLA Modules:
  0.0 35.6 jit_solution(12609534254968884800)
XLA Ops:
  0.6 1.2 %pad.4.tw_ref = f32[1,128]{1,0:T(1,128)} pad(f32[1,32]{1,0:T(1,128)} %bitcast.2, f32[]{:T(128)} %constant.2.clone.1), padding=0_0x0_96 | pad | bytes 644 | tf_op jit(solution)/shard_map/jit(_pad)/pad | solution.py:368
  1.8 31.1 %shard_map.68 = (f32[1,4]{1,0:T(1,128)}, f32[4,8192]{1,0:T(4,128)}) custom-call(bf16[4,16384]{1,0:T(4,128)(2,1)} %th_hbm.1, bf16[4,8192]{1,0:T(4,128)(2,1)} %sh_hbm.1, f32[1,128]{1,0:T(1,128)} %pad.4.tw_ref, bf16[16384,256]{1,0:T(8,128)(2,1)} %thead_hbm.1, bf16[8192,256]{1,0:T(8,128)(2,1)} %shead_hbm.1), custom_call_target="tpu_custom_call" | custom-call | tf_op jit(solution)/shard_map/pallas_call | solution.py:372
  32.9 1.2 %copy.9 = f32[4]{0:T(128)} copy(f32[4]{0:T(128)} %bitcast.3) | data formatting | bytes 32
  34.0 1.6 %copy.10 = f32[4,8192]{1,0:T(4,128)} copy(f32[4,8192]{1,0:T(4,128)} %get-tuple-element.9) | data formatting | bytes 262144

commit v2 on v1

--- a/solution.py
+++ b/solution.py
@@ -37,8 +37,6 @@
     part,
     sbuf,
     rbuf,
-    fbuf,
-    pbuf,
     in_sem,
     thead_sem,
     phead_sem,
@@ -48,7 +46,6 @@
     logit_sem,
     stat_sem,
     red_sem,
-    fin_sem,
 ):
     n1, n2, chunks, red_width = dims
     nchips = n1 * n2
@@ -70,7 +67,7 @@
     def device(v, s, c):
         return {"vocab": v * CORES + c, "section": s}
 
-    sends = []
+    sends, early = [], []
 
     def push(src, dst, recv, target):
         copy = pltpu.make_async_remote_copy(
@@ -109,16 +106,6 @@
     load_s = pltpu.make_async_copy(sh_hbm, sh_in, in_sem.at[1])
     load_t.start()
     load_s.start()
-    loads = {}
-    for index, (is_teacher, first, size, _) in enumerate(chunks):
-        src, dst = (thead_hbm, thead) if is_teacher else (shead_hbm, shead)
-        depth = (kt if is_teacher else ks) // fold
-        for q in range(fold):
-            span = pl.ds(q * depth + first, size)
-            copy = pltpu.make_async_copy(src.at[span], dst.at[span], thead_sem.at[index, q])
-            copy.start()
-            loads[index, q] = copy
-
     load_t.wait()
     load_s.wait()
     for src, dst in ((th_in, gt), (sh_in, gs)):
@@ -132,7 +119,11 @@
     row_chip, row_core, row_token = row // pair_rows, row % pair_rows // rows, row % rows
     source = ((row_chip // n2 * CORES + row_core) * n2 + row_chip % n2) * rows + row_token
     weight = jnp.sum(
-        jnp.where(source == lane, jnp.broadcast_to(tw_ref[...], (tokens, width)), 0.0),
+        jnp.where(
+            source[:, :tokens] == lane[:, :tokens],
+            jnp.broadcast_to(tw_ref[...], (tokens, tokens)),
+            0.0,
+        ),
         axis=1,
         keepdims=True,
     )
@@ -154,38 +145,59 @@
     count = len(chunks)
     along_v = [(v + dv) % n1 for dv in range(1, n1)]
     along_s = [(s + ds) % n2 for ds in range(1, n2)]
-    for i in range(count):
-        for h in range(2):
-            ref, sem = piece(i, slot, h), piece_sem.at[2 * i + h, slot]
-            first = [device(to, s, c) for to in along_v]
-            second = [device(v, to, c) for to in along_s]
-            for target in first + second:
-                push(ref, ref, sem, target)
-        push(whole(i, slot), whole(i, slot), pair_sem.at[i, slot], device(v, s, other))
-    push(
-        shead_hbm.at[pl.ds(pl.multiple_of(other * half, half), half)],
-        phead,
-        phead_sem,
-        device(v, s, other),
-    )
-    for i in range(count):
-        for h in range(2):
+    for turn in range(2):
+        begun = len(sends)
+        for i in range(count):
+            for h, targets in (
+                (turn, [device(to, s, c) for to in along_v]),
+                (1 - turn, [device(v, to, c) for to in along_s]),
+            ):
+                ref, sem = piece(i, slot, h), piece_sem.at[2 * i + h, slot]
+                for target in targets:
+                    push(ref, ref, sem, target)
+        if turn == 0:
+            for copy in sends[begun:]:
+                early.append(copy)
+            loads = {}
+            for index, (is_teacher, first, size, _) in enumerate(chunks):
+                src, dst = (thead_hbm, thead) if is_teacher else (shead_hbm, shead)
+                depth = (kt if is_teacher else ks) // fold
+                for q in range(fold):
+                    span = pl.ds(q * depth + first, size)
+                    copy = pltpu.make_async_copy(src.at[span], dst.at[span], thead_sem.at[index, q])
+                    copy.start()
+                    loads[index, q] = copy
+            for i in range(count):
+                push(whole(i, slot), whole(i, slot), pair_sem.at[i, slot], device(v, s, other))
+            push(
+                shead_hbm.at[pl.ds(pl.multiple_of(other * half, half), half)],
+                phead,
+                phead_sem,
+                device(v, s, other),
+            )
+            for copy in early:
+                copy.wait_send()
+    for turn in range(2):
+        for i in range(count):
             for frm in along_v:
                 at = slot_of(frm, s, c)
-                ref, sem = piece(i, at, h), piece_sem.at[2 * i + h, at]
+                ref, sem = piece(i, at, turn), piece_sem.at[2 * i + turn, at]
                 arrive(ref, sem)
-                if h == 0:
+                if turn == 0:
                     for to in along_s:
                         push(ref, ref, sem, device(v, to, c))
             for frm in along_s:
                 at = slot_of(v, frm, c)
-                ref, sem = piece(i, at, h), piece_sem.at[2 * i + h, at]
+                ref, sem = piece(i, at, 1 - turn), piece_sem.at[2 * i + 1 - turn, at]
                 arrive(ref, sem)
-                if h == 1:
+                if turn == 0:
                     for to in along_v:
                         push(ref, ref, sem, device(to, s, c))
-        for at in [slot_of(frm, s, c) for frm in along_v] + [slot_of(v, frm, c) for frm in along_s]:
-            push(whole(i, at), whole(i, at), pair_sem.at[i, at], device(v, s, other))
+            if turn == 1:
+                for at in [slot_of(frm, s, c) for frm in along_v] + [
+                    slot_of(v, frm, c) for frm in along_s
+                ]:
+                    push(whole(i, at), whole(i, at), pair_sem.at[i, at], device(v, s, other))
 
     block = min(BLOCK, n)
     row_part = lax.broadcasted_iota(jnp.int32, (block * PACK, acc_t.shape[1]), 0) % PACK // rows
@@ -285,6 +297,13 @@
         grads.append((weight * diff).astype(jnp.bfloat16))
 
     steps = half // red_width
+    narrow = red_width // fold
+
+    def fold_rows(x):
+        return jnp.concatenate(
+            [x[:, :, q * narrow : (q + 1) * narrow] for q in range(fold)], axis=1
+        )
+
     nt = (((1,), (1,)), ((), ()))
     for j in range(steps):
         mine = pl.ds(pl.multiple_of(c * half + j * red_width, red_width), red_width)
@@ -296,49 +315,48 @@
             preferred_element_type=F32,
         )
         total = total.reshape(nchips, pair_rows, red_width)
-        part[:, :, j * red_width : (j + 1) * red_width] = total
-        packed = jnp.concatenate(
-            [total[:, :, : red_width // 2], total[:, :, red_width // 2 :]], axis=1
-        )
-        sbuf[:, j] = packed.astype(jnp.bfloat16)
+        packed = [fold_rows(total[:, d * rows : (d + 1) * rows]) for d in range(CORES)]
+        part[:, j] = jnp.where(c == 0, packed[0], packed[1])
+        for d in range(CORES):
+            sbuf[:, d, j] = packed[d].astype(jnp.bfloat16)
         for dv in reversed(range(n1)):
             for ds in reversed(range(n2)):
-                if dv or ds:
-                    tv, ts = (v + dv) % n1, (s + ds) % n2
-                    push(
-                        sbuf.at[tv * n2 + ts, j],
-                        rbuf.at[chip, j],
-                        red_sem.at[chip, j],
-                        device(tv, ts, c),
-                    )
+                for d in (c, other):
+                    if dv or ds or d is other:
+                        tv, ts = (v + dv) % n1, (s + ds) % n2
+                        push(
+                            sbuf.at[tv * n2 + ts, d, j],
+                            rbuf.at[slot, j],
+                            red_sem.at[slot, j],
+                            device(tv, ts, d),
+                        )
 
     kl_rows = column(kl)
     kl_ref[...] = jnp.sum(jnp.where(row == slot * rows + lane, kl_rows, 0.0), axis=0, keepdims=True)[
         :, :rows
     ]
 
-    def pick(value, which):
-        return jnp.where(which == 0, value[:rows], value[rows:])
-
     for j in range(steps):
-        total = part[chip, :, j * red_width : (j + 1) * red_width]
-        for dv in range(n1):
-            for ds in range(n2):
-                if dv or ds:
-                    at = (v + dv) % n1 * n2 + (s + ds) % n2
-                    arrive(rbuf.at[at, j], red_sem.at[at, j])
-                    got = rbuf[at, j].astype(F32)
-                    total += jnp.concatenate([got[:pair_rows], got[pair_rows:]], axis=1)
-        fbuf[j] = total
-        push(fbuf.at[j], pbuf.at[j], fin_sem.at[j], device(v, s, other))
-        to = pl.multiple_of(c * half + j * red_width, red_width)
-        grad_ref[:, pl.ds(to, red_width)] = pick(total, c)
-    for j in range(steps):
-        arrive(pbuf.at[j], fin_sem.at[j])
-        to = pl.multiple_of(other * half + j * red_width, red_width)
-        grad_ref[:, pl.ds(to, red_width)] = pick(pbuf[j], c)
+        for d in (c, other):
+            total = part[chip, j] if d is c else None
+            for dv in range(n1):
+                for ds in range(n2):
+                    if dv or ds or d is other:
+                        at = slot_of((v + dv) % n1, (s + ds) % n2, d)
+                        arrive(rbuf.at[at, j], red_sem.at[at, j])
+                        got = rbuf[at, j].astype(F32)
+                        total = got if total is None else total + got
+            for q in range(fold):
+                to = pl.multiple_of(d * half + j * red_width + q * narrow, narrow)
+                grad_ref[:, pl.ds(to, narrow)] = total[q * rows : (q + 1) * rows]
     for copy in sends:
-        copy.wait_send()
+        if not any(copy is done for done in early):
+            copy.wait_send()
+
+
+def deliver(kl_in, grad_in, kl_ref, grad_ref):
+    kl_ref[...] = kl_in[...]
+    grad_ref[...] = grad_in[...]
 
 
 def shards(n1, n2, th, sh, thead, shead, tw):
@@ -363,10 +381,10 @@
     own = (n1 - 1) + (n2 - 1)
     diagonal = (n1 - 1) * (n2 - 1)
     n_sends = (
-        count * (2 * own + 2 * diagonal + nchips) + 2 + (n - 1) + steps * (nchips - 1) + steps
-    )
-    line = jnp.pad(tw.reshape(1, tokens), ((0, 0), (0, width - tokens)))
-    vmem, anywhere = pl.BlockSpec(memory_space=pltpu.VMEM), pl.BlockSpec(memory_space=pl.ANY)
+        count * (2 * own + 2 * diagonal + nchips) + 2 + (n - 1) + steps * (n - 1)
+    )
+    line = tw.reshape(1, tokens)
+    vmem, anywhere = pl.BlockSpec(memory_space=pltpu.VMEM), pl.BlockSpec(memory_space=pltpu.HBM)
     dma = pltpu.SemaphoreType.DMA
     bf16 = jnp.bfloat16
     kl, grad = pl.pallas_call(
@@ -390,11 +408,9 @@
             pltpu.VMEM((2, tokens, cols), F32),
             pltpu.VMEM((2, tokens, cols), F32),
             pltpu.VMEM((n, 8, width), F32),
-            pltpu.VMEM((nchips, CORES * rows, half), F32),
-            pltpu.VMEM((nchips, steps, PACK, red_width // 2), bf16),
-            pltpu.VMEM((nchips, steps, PACK, red_width // 2), bf16),
-            pltpu.VMEM((steps, CORES * rows, red_width), F32),
-            pltpu.VMEM((steps, CORES * rows, red_width), F32),
+            pltpu.VMEM((nchips, steps, PACK, red_width // fold), F32),
+            pltpu.VMEM((nchips, CORES, steps, PACK, red_width // fold), bf16),
+            pltpu.VMEM((n, steps, PACK, red_width // fold), bf16),
             dma((2,)),
             dma((count, fold)),
             dma,
@@ -403,13 +419,21 @@
             dma((count, n)),
             dma,
             dma((n,)),
-            dma((nchips, steps)),
-            dma((steps,)),
+            dma((n, steps)),
         ],
         compiler_params=pltpu.CompilerParams(
             collective_id=0, has_side_effects=True, vmem_limit_bytes=60 * 1024 * 1024
         ),
     )(th, sh, line, thead, shead)
+    kl, grad = pl.pallas_call(
+        deliver,
+        out_shape=(
+            jax.ShapeDtypeStruct((1, rows), F32),
+            jax.ShapeDtypeStruct((rows, ks), F32),
+        ),
+        in_specs=[vmem, vmem],
+        out_specs=(vmem, vmem),
+    )(kl, grad)
     return kl.reshape(rows), grad
 
 

time: 35.8 us -> 30.2 us (0.84)
  local copies, waits for them, and re-layouts: 3.91 us -> 0 us
  Pallas kernels: 31.1 us -> 29.4 us
    pallas_call x1, Pallas kernels: 31.1 us -> 27.8 us  [shards(): pl.pallas_call(functools.partial(kernel, (n1, n2, chunks, red_width)), ou...]
    unnamed x2 -> x0, local copies, waits for them, and re-layouts: 2.74 us -> none
    pallas_call x0 -> x1, Pallas kernels: none -> 1.58 us  [shards(): pl.pallas_call(deliver, out_shape=(jax.ShapeDtypeStruct((1, rows), F32),...]
    pad x1 -> x0, local copies, waits for them, and re-layouts: 1.17 us -> none  [shards(): line = jnp.pad(tw.reshape(1, tokens), ((0, 0), (0, width - tokens)))]
where the time goes in v2:
time: 30.2 us; the launch traced here: 30.1 us
  Pallas kernels  29.4 us (97%)
  between operations  0.64 us (2%)
    pallas_call x1, Pallas kernels, shards(): pl.pallas_call(functools.partial(kernel, (n1, n2, chunks, red_width)), ou...  27.8 us
    pallas_call x1, Pallas kernels, shards(): pl.pallas_call(deliver, out_shape=(jax.ShapeDtypeStruct((1, rows), F32),...  1.58 us

profile of v2, /device:TPU:0, one launch (start us, length us, event | category | flops | bytes accessed | tf_op | source)
XLA Modules:
  0.0 30.1 jit_solution(539127862634602032)
XLA Ops:
  0.6 27.8 %shard_map.68 = (f32[1,4]{1,0:T(1,128)}, f32[4,8192]{1,0:T(4,128)}) custom-call(bf16[4,16384]{1,0:T(4,128)(2,1)} %th_hbm.1, bf16[4,8192]{1,0:T(4,128)(2,1)} %sh_hbm.1, f32[1,32]{1,0:T(1,128)} %bitcast.2, bf16[16384,256]{1,0:T(8,128)(2,1)} %thead_hbm.1, bf16[8192,256]{1,0:T(8,128)(2,1)} %shead_hbm.1), custom_call_target="tpu_custom_call" | custom-call | tf_op jit(solution)/shard_map/pallas_call | solution.py:390
  28.5 1.6 %shard_map.69 = (f32[1,4]{1,0:T(1,128)}, f32[4,8192]{1,0:T(4,128)}) custom-call(f32[1,4]{1,0:T(1,128)} %get-tuple-element.6.kl_in, f32[4,8192]{1,0:T(4,128)} %get-tuple-element.7.grad_in), custom_call_target="tpu_custom_call" | custom-call | tf_op jit(solution)/shard_map/pallas_call | solution.py:428

commit v3 on v2

--- a/solution.py
+++ b/solution.py
@@ -375,7 +375,7 @@
         (False, 0, sd, True),
     )
     half = ks // CORES
-    steps = 4
+    steps = 2
     red_width = half // steps
     count = len(chunks)
     own = (n1 - 1) + (n2 - 1)
@@ -389,10 +389,7 @@
     bf16 = jnp.bfloat16
     kl, grad = pl.pallas_call(
         functools.partial(kernel, (n1, n2, chunks, red_width)),
-        out_shape=(
-            jax.ShapeDtypeStruct((1, rows), F32),
-            jax.ShapeDtypeStruct((rows, ks), F32),
-        ),
+        out_shape=(pltpu.VMEM((1, rows), F32), pltpu.VMEM((rows, ks), F32)),
         in_specs=[anywhere, anywhere, vmem, anywhere, anywhere],
         out_specs=(vmem, vmem),
         scratch_shapes=[
@@ -433,6 +430,7 @@
         ),
         in_specs=[vmem, vmem],
         out_specs=(vmem, vmem),
+        compiler_params=pltpu.CompilerParams(vmem_limit_bytes=4 * 1024 * 1024),
     )(kl, grad)
     return kl.reshape(rows), grad
 

time: 30.2 us -> 28.4 us (0.940)
  Pallas kernels: 29.4 us -> 27.6 us
    pallas_call x1, Pallas kernels: 27.8 us -> 26.9 us  [shards(): pl.pallas_call(functools.partial(kernel, (n1, n2, chunks, red_width)), ou...]
    pallas_call x1, Pallas kernels: 1.58 us -> 0.67 us  [shards(): pl.pallas_call(deliver, out_shape=(jax.ShapeDtypeStruct((1, rows), F32),...]
where the time goes in v3:
time: 28.4 us; the launch traced here: 28.2 us
  Pallas kernels  27.6 us (97%)
  between operations  0.64 us (2%)
    pallas_call x1, Pallas kernels, shards(): pl.pallas_call(functools.partial(kernel, (n1, n2, chunks, red_width)), ou...  26.9 us
    pallas_call x1, Pallas kernels, shards(): pl.pallas_call(deliver, out_shape=(jax.ShapeDtypeStruct((1, rows), F32),...  0.67 us

profile of v3, /device:TPU:0, one launch (start us, length us, event | category | flops | bytes accessed | tf_op | source)
XLA Modules:
  0.0 28.2 jit_solution(14521741039768788305)
XLA Ops:
  0.6 26.9 %shard_map.68 = (f32[1,4]{1,0:T(1,128)S(1)}, f32[4,8192]{1,0:T(4,128)S(1)}) custom-call(bf16[4,16384]{1,0:T(4,128)(2,1)} %th_hbm.1, bf16[4,8192]{1,0:T(4,128)(2,1)} %sh_hbm.1, f32[1,32]{1,0:T(1,128)} %bitcast.2, bf16[16384,256]{1,0:T(8,128)(2,1)} %thead_hbm.1, bf16[8192,256]{1,0:T(8,128)(2,1)} %shead_hbm.1), custom_call_target="tpu_custom_call" | custom-call | tf_op jit(solution)/shard_map/pallas_call | solution.py:390
  27.5 0.7 %shard_map.69 = (f32[1,4]{1,0:T(1,128)}, f32[4,8192]{1,0:T(4,128)}) custom-call(f32[1,4]{1,0:T(1,128)S(1)} %get-tuple-element.6.kl_in, f32[4,8192]{1,0:T(4,128)S(1)} %get-tuple-element.7.grad_in), custom_call_target="tpu_custom_call" | custom-call | tf_op jit(solution)/shard_map/pallas_call | solution.py:425
